TPU v7x, 32 devices: a whole 2x2x4 slice. The times are simulated.
32 devices in a mesh: group: 2 (over y), section: 4 (over x, core), tensor: 4 (over z).
Axes of the slice: x: 2, y: 2, z: 4, core: 2. Of those that a mesh axis runs over, the one named last changes fastest.
Arguments:
- hidden_states: bfloat16 [2, 4, 4, 8192], P('group', 'section', 'tensor'), may hold values from -6 to 6
- query_train: bfloat16 [4, 8192, 4096], P(None, ('group', 'section'), 'tensor'), may hold values from -0.0625 to 0.0625
- keyval_train: bfloat16 [4, 8192, 1024], P(None, ('group', 'section'), 'tensor'), may hold values from -0.0625 to 0.0625
- layer_of_section: int32 [4], replicated, may hold values from 0 to 3, each once
- lengths: int32 [2, 4, 4], P('group', 'section', 'tensor'), may hold values from 2 to 1024
- kv_cache: bfloat16 [2, 4, 4, 1024, 1024], P('group', 'section', 'tensor'), as said below
Outputs:
- attended: bfloat16 [2, 4, 4, 4096], P('group', 'section', 'tensor')
- new_entries: bfloat16 [2, 4, 4, 1024], P('group', 'section', 'tensor')
Inputs may be any that keep to these rules, and one draw needn't show every extreme that they name: `layer_of_section`: every layer appears once. `kv_cache`: cache positions at or past a sequence's length hold entries that are never read.
All inputs are finite; a program needn't handle non-finite values.
Results may differ from a plain program's by a relative error of at most 0.03.
Values may be sent and summed in bfloat16 or wider, within the bound.
A program may use at most 64 MiB of HBM per device.

v0:
```python
import jax
import jax.numpy as jnp
from jax import lax
from jax.sharding import PartitionSpec as P

HD = 128
QH = 32
KVH = 4


def rotate(vectors, position):
    half_size = HD // 2
    inverse = jnp.power(jnp.float32(500000.0), -jnp.arange(half_size, dtype=jnp.float32) * 2.0 / HD)
    angle = position[:, None, None] * inverse[None, None, :]
    cosine = jnp.cos(angle)
    sine_part = jnp.sin(angle)
    first_half = vectors[..., :half_size]
    second = vectors[..., half_size:]
    return jnp.concatenate(
        [first_half * cosine - second * sine_part, second * cosine + first_half * sine_part],
        axis=-1,
    )


def attend(queries, key_value, seq_lens, cache):
    count = queries.shape[0]
    cache_len = cache.shape[1]
    per_kv = QH // KVH
    position = seq_lens.astype(jnp.float32)
    query_rot = rotate(queries.astype(jnp.float32).reshape(count, QH, HD), position).astype(
        jnp.bfloat16
    )
    key_rot = rotate(
        key_value[:, : KVH * HD].astype(jnp.float32).reshape(count, KVH, HD), position
    ).astype(jnp.bfloat16)
    new_values = key_value[:, KVH * HD :]
    cache_keys = cache[:, :, : KVH * HD].reshape(count, cache_len, KVH, HD)
    cache_values = cache[:, :, KVH * HD :].reshape(count, cache_len, KVH, HD)
    query_group = query_rot.reshape(count, KVH, per_kv, HD)
    score_scale = 1.0 / jnp.sqrt(jnp.float32(HD))
    scores = (
        jnp.einsum("skgd,sjkd->skgj", query_group, cache_keys, preferred_element_type=jnp.float32)
        * score_scale
    )
    own_score = (
        jnp.einsum("skgd,skd->skg", query_group, key_rot, preferred_element_type=jnp.float32)
        * score_scale
    )
    usable = (jnp.arange(cache_len, dtype=jnp.int32)[None, :] < seq_lens[:, None])[:, None, None, :]
    scores = jnp.where(usable, scores, jnp.float32(-1e30))
    largest = jnp.maximum(jnp.max(scores, axis=-1), own_score)
    exponent = jnp.where(usable, jnp.exp(scores - largest[..., None]), jnp.float32(0.0))
    own_exp = jnp.exp(own_score - largest)
    totals = jnp.sum(exponent, axis=-1) + own_exp
    probs = (exponent / totals[..., None]).astype(jnp.bfloat16)
    own_prob = (own_exp / totals).astype(jnp.bfloat16)
    new_float = new_values.astype(jnp.float32).reshape(count, KVH, HD)
    result = jnp.einsum("skgj,sjkd->skgd", probs, cache_values, preferred_element_type=jnp.float32)
    result = result + own_prob.astype(jnp.float32)[..., None] * new_float[:, :, None, :]
    entries = jnp.concatenate([key_rot.reshape(count, KVH * HD), new_values], axis=1)
    return (result.reshape(count, QH * HD).astype(jnp.bfloat16), entries)


def shards(hidden_states, query_train, keyval_train, layer_of_section, lengths, kv_cache):
    all_tokens = lax.all_gather(hidden_states[0, 0], "tensor", axis=0, tiled=True)
    query_sorted = query_train[layer_of_section]
    keyval_sorted = keyval_train[layer_of_section]
    moved = (
        lax.all_to_all(query_sorted, "section", split_axis=0, concat_axis=1, tiled=True),
        lax.all_to_all(keyval_sorted, "section", split_axis=0, concat_axis=1, tiled=True),
    )
    query_cols = moved[0].shape[2]
    batch_rows = all_tokens.shape[0]
    group_count = lax.axis_size("group")
    row_count = moved[0].shape[1]
    blocks = all_tokens.reshape(1, batch_rows, group_count, row_count)
    arrived = lax.all_to_all(blocks, "group", split_axis=2, concat_axis=0, tiled=True)
    w_both = jnp.concatenate([moved[0][0], moved[1][0]], axis=1)
    both_parts = lax.psum_scatter(
        jnp.einsum("gbr,rc->gbc", arrived[:, :, 0, :], w_both, preferred_element_type=jnp.float32),
        "group",
        scatter_dimension=0,
        tiled=True,
    )[0]
    query_part = both_parts[:, :query_cols]
    keyval_part = both_parts[:, query_cols:]
    queries = query_part.astype(jnp.bfloat16)
    key_value = keyval_part.astype(jnp.bfloat16)
    query_seq, keyval_seq = (
        lax.all_to_all(queries, "tensor", split_axis=0, concat_axis=1, tiled=True),
        lax.all_to_all(key_value, "tensor", split_axis=0, concat_axis=1, tiled=True),
    )
    result, entries = attend(query_seq, keyval_seq, lengths[0, 0], kv_cache[0, 0])
    return (result[None, None], entries[None, None])


def solution(mesh):
    in_specs = (
        P("group", "section", "tensor", None),
        P(None, ("group", "section"), "tensor"),
        P(None, ("group", "section"), "tensor"),
        P(),
        P("group", "section", "tensor"),
        P("group", "section", "tensor", None, None),
    )
    out_specs = (P("group", "section", "tensor", None), P("group", "section", "tensor", None))
    return jax.shard_map(shards, mesh=mesh, in_specs=in_specs, out_specs=out_specs, check_vma=False)
```

profile of v0, /device:TPU:0, one launch (start us, length us, event | category | flops | bytes accessed | tf_op | source)
XLA Modules:
  0.0 190.8 jit_solution(7543319990391198501)
XLA Ops:
  0.6 0.0 copy-start
  0.6 15.4 %all-gather = bf16[4,1,1,8192]{3,2,1,0:T(2,128)(2,1)S(1)} all-gather(bf16[1,1,1,8192]{3,2,1,0:T(2,128)(2,1)} %param.6), channel_id=2, replica_groups=mesh['group'=2,'section'=4,'tensor'=4] {'tensor'}, dimensions={0}, use_global_device_ids=true | all-gather | bytes 81920 | tf_op jit(solution)/shard_map/all_gather | solution.py:65
  16.1 1.0 reduce.4
  17.1 3.3 %all-to-all-start.2 = ((bf16[1,4,2,4096]{3,1,0,2:T(4,128)(2,1)}), bf16[1,4,2,4096]{3,1,0,2:T(4,128)(2,1)S(1)}, u32[]{:S(2)}, u32[]{:S(2)}) async-start(bf16[1,4,2,4096]{3,1,0,2:T(4,128)(2,1)} %bitcast.30), calls=%async_computation.2 | async-start | bytes 131072 | tf_op jit(solution)/shard_map/all_to_all | solution.py:77
  20.4 0.7 compare_select_fusion
  21.0 0.0 copy-done
  21.1 2.0 %gather_fusion = bf16[4,1024,256]{2,1,0:T(8,128)(2,1)} fusion(bf16[4,1024,256]{2,1,0:T(8,128)(2,1)S(1)} %copy-done, s32[1024]{0:T(1024)S(1)} %pad_clamp_fusion), kind=kCustom, calls=%fused_computation | custom fusion | bytes 4194320 | tf_op jit(solution)/shard_map/gather | solution.py:67
  23.0 1.4 all-to-all-done.2
  24.5 4.4 %all-to-all-start.1 = ((bf16[4,1024,256]{2,1,0:T(8,128)(2,1)}), bf16[4,1024,256]{2,1,0:T(8,128)(2,1)}, u32[]{:S(2)}, u32[]{:S(2)}) async-start(bf16[4,1024,256]{2,1,0:T(8,128)(2,1)} %gather_fusion), calls=%async_computation.1 | async-start | bytes 4194304 | tf_op jit(solution)/shard_map/all_to_all | solution.py:70
  28.9 5.9 %fusion.23 = (bf16[4,512,1024]{2,1,0:T(8,128)(2,1)}, bf16[4,512,1024]{2,1,0:T(8,128)(2,1)}) fusion(bf16[4,1024,1024]{2,1,0:T(8,128)(2,1)} %param.7), kind=kLoop, calls=%fused_computation.53 | loop fusion | bytes 16777216 | tf_op jit(solution)/shard_map/gather | solution.py:66
  34.8 5.0 %gather_fusion.1 = bf16[4,512,1024]{2,1,0:T(8,128)(2,1)} fusion(bf16[4,512,1024]{2,1,0:T(8,128)(2,1)} %get-tuple-element.2, s32[1024]{0:T(1024)S(1)} %pad_clamp_fusion), kind=kCustom, calls=%fused_computation.1 | custom fusion | bytes 8388624 | tf_op jit(solution)/shard_map/gather | solution.py:66
  39.8 4.9 %gather_fusion.2 = bf16[4,512,1024]{2,1,0:T(8,128)(2,1)} fusion(bf16[4,512,1024]{2,1,0:T(8,128)(2,1)} %get-tuple-element.3, s32[1024]{0:T(1024)S(1)} %pad_clamp_fusion), kind=kCustom, calls=%fused_computation.2 | custom fusion | bytes 8388624 | tf_op jit(solution)/shard_map/gather | solution.py:66
  44.7 7.7 %pad_maximum_fusion = bf16[4,1024,1024]{2,1,0:T(8,128)(2,1)} fusion(bf16[4,512,1024]{2,1,0:T(8,128)(2,1)} %gather_fusion.2, bf16[4,512,1024]{2,1,0:T(8,128)(2,1)} %gather_fusion.1), kind=kLoop, calls=%fused_computation.5 | loop fusion | flops 16777216 | bytes 16777216
  52.4 2.3 %all-to-all-done.1 = bf16[4,1024,256]{2,1,0:T(8,128)(2,1)} async-done(((bf16[4,1024,256]{2,1,0:T(8,128)(2,1)}), bf16[4,1024,256]{2,1,0:T(8,128)(2,1)}, u32[]{:S(2)}, u32[]{:S(2)}) %all-to-all-start.1) | async-done | bytes 2097184 | tf_op jit(solution)/shard_map/all_to_all | solution.py:70
  54.7 5.7 %all-to-all-start = ((bf16[4,1024,1024]{2,1,0:T(8,128)(2,1)}), bf16[4,1024,1024]{2,1,0:T(8,128)(2,1)}, u32[]{:S(2)}, u32[]{:S(2)}) async-start(bf16[4,1024,1024]{2,1,0:T(8,128)(2,1)} %pad_maximum_fusion), calls=%async_computation | async-start | bytes 16777216 | tf_op jit(solution)/shard_map/all_to_all | solution.py:69
  60.4 0.0 copy-start.1
  61.0 3.9 %copy.14 = bf16[1,1,1,1024,1024]{3,4,2,1,0:T(8,128)(2,1)} copy(bf16[1,1,1,1024,1024]{4,3,2,1,0:T(8,128)(2,1)} %param.11) | data formatting | bytes 4194304 | tf_op args[5]
  65.0 0.0 copy-done.1
  65.0 0.6 dynamic-slice
  65.6 2.7 %fusion.24 = (bf16[1,1024,512]{1,2,0:T(8,128)(2,1)}, bf16[1,1024,512]{1,2,0:T(8,128)(2,1)S(1)}) fusion(bf16[1,1024,1024]{1,2,0:T(8,128)(2,1)} %bitcast.53), kind=kLoop, calls=%fused_computation.54 | loop fusion | bytes 4194304 | tf_op jit(solution)/shard_map/slice | solution.py:37
  68.3 85.2 %all-to-all-done = bf16[4,1024,1024]{2,1,0:T(8,128)(2,1)} async-done(((bf16[4,1024,1024]{2,1,0:T(8,128)(2,1)}), bf16[4,1024,1024]{2,1,0:T(8,128)(2,1)}, u32[]{:S(2)}, u32[]{:S(2)}) %all-to-all-start) | async-done | bytes 8388640 | tf_op jit(solution)/shard_map/all_to_all | solution.py:69
  153.5 4.9 %fusion.1 = f32[2,4,1280]{2,1,0:T(4,128)S(1)} fusion(bf16[4096,256]{1,0:T(8,128)(2,1)} %bitcast.2, bf16[4096,1024]{1,0:T(8,128)(2,1)} %bitcast.1, bf16[1,4,2,4096]{3,1,0,2:T(4,128)(2,1)S(1)} %all-to-all-done.2), kind=kOutput, calls=%fused_computation.6 | convolution fusion | flops 104857600 | bytes 10592256 | tf_op jit(solution)/shard_map/gbr,rc->gbc/dot_general | solution.py:80
  158.4 7.6 %all-reduce = bf16[2,4,1280]{2,1,0:T(4,128)(2,1)S(1)} all-reduce(f32[2,4,1280]{2,1,0:T(4,128)S(1)} %fusion.1), channel_id=3, replica_groups=mesh['group'=2,'section'=4,'tensor'=4] {'group'}, use_global_device_ids=true, to_apply=%region_0.0.clone | all-reduce | flops 10240 | bytes 61440
  165.9 0.7 fusion.10
  166.6 0.5 broadcast.87
  167.1 0.7 reduce.6
  167.8 0.6 reshape.255
  168.4 5.0 %all-to-all-start.4 = ((bf16[4,2,128]{2,1,0:T(2,128)(2,1)}), bf16[4,2,128]{2,1,0:T(2,128)(2,1)S(1)}, u32[]{:S(2)}, u32[]{:S(2)}) async-start(bf16[4,2,128]{2,1,0:T(2,128)(2,1)} %reshape.255), calls=%async_computation.4 | async-start | bytes 4096 | tf_op jit(solution)/shard_map/all_to_all | solution.py:91
  173.3 0.7 reduce.5
  174.0 0.6 reshape.253
  174.6 4.2 %all-to-all-done.4 = bf16[4,2,128]{2,1,0:T(2,128)(2,1)S(1)} async-done(((bf16[4,2,128]{2,1,0:T(2,128)(2,1)}), bf16[4,2,128]{2,1,0:T(2,128)(2,1)S(1)}, u32[]{:S(2)}, u32[]{:S(2)}) %all-to-all-start.4) | async-done | bytes 2080 | tf_op jit(solution)/shard_map/all_to_all | solution.py:91
  178.8 3.2 %all-to-all-start.3 = ((bf16[4,2,512]{2,1,0:T(2,128)(2,1)}), bf16[4,2,512]{2,1,0:T(2,128)(2,1)S(1)}, u32[]{:S(2)}, u32[]{:S(2)}) async-start(bf16[4,2,512]{2,1,0:T(2,128)(2,1)} %reshape.253), calls=%async_computation.3 | async-start | bytes 16384 | tf_op jit(solution)/shard_map/all_to_all | solution.py:90
  182.1 0.1 subtract_convert_fusion.1
  182.2 0.1 maximum_bitcast_fusion.6
  182.3 0.6 maximum_bitcast_fusion.4
  182.9 0.1 maximum_bitcast_fusion.5
  183.0 4.7 %all-to-all-done.3 = bf16[4,2,512]{2,1,0:T(2,128)(2,1)S(1)} async-done(((bf16[4,2,512]{2,1,0:T(2,128)(2,1)}), bf16[4,2,512]{2,1,0:T(2,128)(2,1)S(1)}, u32[]{:S(2)}, u32[]{:S(2)}) %all-to-all-start.3) | async-done | bytes 8224 | tf_op jit(solution)/shard_map/all_to_all | solution.py:90
  187.7 0.1 fusion.11
  187.8 0.2 fusion.13
  188.0 1.6 fusion.26
  189.6 0.2 fusion.4
  189.8 0.4 fusion.3
  190.2 0.6 convert_element_type.77
  (12 shorter events, 0.2 us)
Async XLA Ops:
  0.6 20.4 %copy-start = (bf16[4,1024,256]{2,1,0:T(8,128)(2,1)S(1)}, bf16[4,1024,256]{2,1,0:T(8,128)(2,1)}, u32[]{:S(2)}) copy-start(bf16[4,1024,256]{2,1,0:T(8,128)(2,1)} %param.8) | copy-start | bytes 6291460
  17.1 7.4 %all-to-all-start.2 = ((bf16[1,4,2,4096]{3,1,0,2:T(4,128)(2,1)}), bf16[1,4,2,4096]{3,1,0,2:T(4,128)(2,1)S(1)}, u32[]{:S(2)}, u32[]{:S(2)}) async-start(bf16[1,4,2,4096]{3,1,0,2:T(4,128)(2,1)} %bitcast.30), calls=%async_computation.2 | async-start | bytes 131072 | tf_op jit(solution)/shard_map/all_to_all | solution.py:77
  24.5 30.2 %all-to-all-start.1 = ((bf16[4,1024,256]{2,1,0:T(8,128)(2,1)}), bf16[4,1024,256]{2,1,0:T(8,128)(2,1)}, u32[]{:S(2)}, u32[]{:S(2)}) async-start(bf16[4,1024,256]{2,1,0:T(8,128)(2,1)} %gather_fusion), calls=%async_computation.1 | async-start | bytes 4194304 | tf_op jit(solution)/shard_map/all_to_all | solution.py:70
  54.7 98.8 %all-to-all-start = ((bf16[4,1024,1024]{2,1,0:T(8,128)(2,1)}), bf16[4,1024,1024]{2,1,0:T(8,128)(2,1)}, u32[]{:S(2)}, u32[]{:S(2)}) async-start(bf16[4,1024,1024]{2,1,0:T(8,128)(2,1)} %pad_maximum_fusion), calls=%async_computation | async-start | bytes 16777216 | tf_op jit(solution)/shard_map/all_to_all | solution.py:69
  60.4 4.6 %copy-start.1 = (u32[32]{0:T(128)S(1)}, u32[32]{0:T(128)}, u32[]{:S(2)}) copy-start(u32[32]{0:T(128)} %constant.26) | copy-start | bytes 388
  168.4 10.5 %all-to-all-start.4 = ((bf16[4,2,128]{2,1,0:T(2,128)(2,1)}), bf16[4,2,128]{2,1,0:T(2,128)(2,1)S(1)}, u32[]{:S(2)}, u32[]{:S(2)}) async-start(bf16[4,2,128]{2,1,0:T(2,128)(2,1)} %reshape.255), calls=%async_computation.4 | async-start | bytes 4096 | tf_op jit(solution)/shard_map/all_to_all | solution.py:91
  178.8 8.8 %all-to-all-start.3 = ((bf16[4,2,512]{2,1,0:T(2,128)(2,1)}), bf16[4,2,512]{2,1,0:T(2,128)(2,1)S(1)}, u32[]{:S(2)}, u32[]{:S(2)}) async-start(bf16[4,2,512]{2,1,0:T(2,128)(2,1)} %reshape.253), calls=%async_computation.3 | async-start | bytes 16384 | tf_op jit(solution)/shard_map/all_to_all | solution.py:90
where the time goes:
time: 192 us; the launch traced here: 191 us
  waiting for transfers between devices  97.8 us (51%)
  local copies, waits for them, and re-layouts  28.1 us (15%)
  blocking collectives  23 us (12%)
  starting transfers between devices  21.6 us (11%)
  other arithmetic  11.8 us (6%)
  matrix products  7.11 us (4%)
    all_to_all x1, waiting for transfers between devices, shards(): lax.all_to_all(query_sorted, 'section', split_axis=0, concat_axis=1, tile...  85.2 us
    gather x3, local copies, waits for them, and re-layouts, shards(): query_sorted = query_train[layer_of_section]  15.8 us
    all_gather x1, blocking collectives, shards(): lax.all_gather(hidden_states[0, 0], 'tensor', axis=0, tiled=True)  15.4 us
    unnamed x2, other arithmetic  7.75 us
    unnamed x1, blocking collectives  7.55 us
    unnamed x11, local copies, waits for them, and re-layouts  5.77 us
    all_to_all x1, starting transfers between devices, shards(): lax.all_to_all(query_sorted, 'section', split_axis=0, concat_axis=1, tile...  5.67 us
    all_to_all x1, starting transfers between devices, shards(): lax.all_to_all(key_value, 'tensor', split_axis=0, concat_axis=1, tiled=True)  4.97 us
  transfers between devices with their start and end apart: 5, of which 5 were waited for; matrix products, arithmetic and copies ran while one was open for 19% of the time, Pallas kernels for 0%

commit v1 on v0

v1 whole, which is shorter than its diff:
```python
import functools

import jax
import jax.numpy as jnp
from jax import lax
from jax.experimental import pallas as pl
from jax.experimental.pallas import tpu as pltpu
from jax.sharding import PartitionSpec as P

HD = 128
MESH = pl.DeviceIdType.MESH


def kernel(sizes, layer_hbm, len_hbm, h_hbm, wq_hbm, wk_hbm, cache_hbm, out_ref, ent_ref,
           layer_ref, len_ref, h_vm, h_rows, h_pack, x_all, x_rows, wq, wk, cache, send_p, recv_p, send_z, recv_z, heads,
           sem_i, sem_h, sem_w, sem_c, a_send, a_recv, b_send, b_recv, p_send, p_recv, z_send, z_recv):
    n_group, n_section, n_tensor = sizes
    n_plane = n_group * n_section
    g, s, t = lax.axis_index("group"), lax.axis_index("section"), lax.axis_index("tensor")
    me = g * n_section + s
    rows = wq.shape[1]
    q_cols, k_cols = wq.shape[2], wk.shape[2]
    kv_heads = cache.shape[1] // 2 // HD
    q_heads = q_cols * n_tensor // HD
    per_kv = q_heads // kv_heads

    def plane_id(p):
        return (p // n_section, lax.rem(p, n_section), t)

    barrier = pltpu.get_barrier_semaphore()
    plane = [lax.rem(me + k, n_plane) for k in range(1, n_plane)]
    line = [lax.rem(t + k, n_tensor) for k in range(1, n_tensor)]
    for p in plane:
        pl.semaphore_signal(barrier, inc=1, device_id=plane_id(p), device_id_type=MESH)
    for z in line:
        pl.semaphore_signal(barrier, inc=1, device_id=(g, s, z), device_id_type=MESH)

    load_h = pltpu.make_async_copy(h_hbm, h_vm, sem_h)
    load_h.start()
    load_layer = pltpu.make_async_copy(layer_hbm, layer_ref, sem_i.at[0])
    load_len = pltpu.make_async_copy(len_hbm, len_ref, sem_i.at[1])
    load_layer.start()
    load_len.start()
    loads = []
    for l in range(n_section):
        loads.append(pltpu.make_async_copy(wq_hbm.at[l], wq.at[l], sem_w.at[0, l]))
        loads.append(pltpu.make_async_copy(wk_hbm.at[l], wk.at[l], sem_w.at[1, l]))
    load_c = pltpu.make_async_copy(cache_hbm, cache, sem_c)
    for c in loads:
        c.start()
    load_c.start()

    tile = rows // HD
    load_h.wait()
    for j in range(n_plane * tile):
        h_rows[j:j + 1, :] = h_vm[:, j * HD:(j + 1) * HD].astype(jnp.float32)
    for p in range(n_plane):
        h_pack[p] = h_rows[p * tile:(p + 1) * tile, :].astype(jnp.bfloat16)
    x_all[t, me] = h_pack[me]
    load_layer.wait()
    load_len.wait()
    pl.semaphore_wait(barrier, n_plane - 1 + n_tensor - 1)

    def copy_a(p, slot, sem):
        return pltpu.make_async_remote_copy(
            src_ref=h_pack.at[p],
            dst_ref=x_all.at[t, slot],
            send_sem=a_send.at[p], recv_sem=a_recv.at[sem],
            device_id=plane_id(p), device_id_type=MESH)

    for p in plane:
        copy_a(p, me, me).start()

    half = HD // 2
    lane = lax.broadcasted_iota(jnp.int32, (1, HD), 1)
    freq_at = jnp.where(lane < half, lane, lane - half).astype(jnp.float32)
    inverse = jnp.exp(freq_at * jnp.float32(-2.0 / HD) * jnp.log(jnp.float32(500000.0)))
    seq_len = len_ref[0, 0, 0]
    angle = seq_len.astype(jnp.float32) * inverse
    cosine = jnp.cos(angle)
    sine = jnp.where(lane < half, -jnp.sin(angle), jnp.sin(angle))

    for p in plane:
        copy_a(p, p, p).wait_recv()

    def copy_b(z, slot, sem):
        return pltpu.make_async_remote_copy(
            src_ref=x_all.at[t], dst_ref=x_all.at[slot],
            send_sem=b_send.at[z], recv_sem=b_recv.at[sem],
            device_id=(g, s, z), device_id_type=MESH)

    for z in line:
        copy_b(z, t, t).start()

    def place(b):
        for gg in range(n_group):
            for ss in range(n_section):
                at = pl.multiple_of((gg * n_tensor + b) * tile, tile)
                x_rows[ss, pl.ds(at, tile), :] = x_all[b, gg * n_section + ss].astype(jnp.float32)

    place(t)
    for c in loads:
        c.wait()
    for z in line:
        copy_b(z, z, z).wait_recv()
        place(z)

    base = (s // 2) * 2 + 2

    def copy_p(p, slot, sem):
        return pltpu.make_async_remote_copy(
            src_ref=send_p.at[p], dst_ref=recv_p.at[slot],
            send_sem=p_send.at[p], recv_sem=p_recv.at[sem],
            device_id=plane_id(p), device_id_type=MESH)

    def section_step(k, carry):
        ss = lax.rem(base + k, n_section)
        layer = layer_ref[ss]
        tokens = jnp.concatenate(
            [x_rows[ss, pl.ds(i, n_group * n_tensor, stride=tile), :] for i in range(tile)],
            axis=1).astype(jnp.bfloat16)
        part_q = jnp.dot(tokens, wq[layer], preferred_element_type=jnp.float32)
        part_k = jnp.dot(tokens, wk[layer], preferred_element_type=jnp.float32)
        for gg in range(n_group):
            p = gg * n_section + ss
            lo, hi = gg * n_tensor, (gg + 1) * n_tensor
            send_p[p, :, 0:q_cols] = part_q[lo:hi].astype(send_p.dtype)
            send_p[p, :, q_cols:q_cols + k_cols] = part_k[lo:hi].astype(send_p.dtype)

            @pl.when(p != me)
            def _():
                copy_p(p, me, me).start()
        return carry

    lax.fori_loop(0, n_section, section_step, 0)

    total = send_p[me].astype(jnp.float32)
    for p in plane:
        copy_p(p, p, p).wait_recv()
        total += recv_p[p].astype(jnp.float32)

    def copy_z(z, slot, sem):
        return pltpu.make_async_remote_copy(
            src_ref=send_z.at[z], dst_ref=recv_z.at[slot],
            send_sem=z_send.at[z], recv_sem=z_recv.at[sem],
            device_id=(g, s, z), device_id_type=MESH)

    for b in range(n_tensor):
        send_z[b] = total[b:b + 1].astype(jnp.bfloat16)
    for z in line:
        copy_z(z, t, t).start()

    q_per, k_per = q_cols // HD, k_cols // HD

    def spread(src, z):
        row = src.astype(jnp.float32)
        for j in range(q_per):
            heads[pl.ds(z * q_per + j, 1), :] = row[:, j * HD:(j + 1) * HD]
        for j in range(k_per):
            heads[pl.ds(q_heads + z * k_per + j, 1), :] = row[:, q_cols + j * HD:q_cols + (j + 1) * HD]

    spread(send_z[t], t)
    for z in line:
        copy_z(z, z, z).wait_recv()
        spread(recv_z[z], z)
    if k_per == 0:
        for z in range(n_tensor):
            row = jnp.where(t == z, send_z[z], recv_z[z]).astype(jnp.float32)
            at, lo = divmod(z * k_cols, HD)
            heads[q_heads + at:q_heads + at + 1, lo:lo + k_cols] = row[:, q_cols:q_cols + k_cols]

    def rotate(u):
        return (u * cosine + pltpu.roll(u, half, 1) * sine).astype(jnp.bfloat16)

    query_rot = rotate(heads[0:q_heads])
    key_rot = rotate(heads[q_heads:q_heads + kv_heads])
    new_value = heads[q_heads + kv_heads:q_heads + 2 * kv_heads]
    for j in range(kv_heads):
        ent_ref[0, 0, :, j * HD:(j + 1) * HD] = key_rot[j:j + 1].astype(jnp.float32).astype(jnp.bfloat16)
        at = (kv_heads + j) * HD
        ent_ref[0, 0, :, at:at + HD] = new_value[j:j + 1].astype(jnp.bfloat16)

    def per_query(u):
        return jnp.concatenate(
            [jnp.broadcast_to(u[k:k + 1], (per_kv, HD)) for k in range(kv_heads)], axis=0)

    scale = 1.0 / jnp.sqrt(jnp.float32(HD))
    query_float = query_rot.astype(jnp.float32)
    own_score = jnp.sum(query_float * per_query(key_rot.astype(jnp.float32)), axis=1, keepdims=True) * scale
    head_row = lax.broadcasted_iota(jnp.int32, (q_heads, HD), 0) // per_kv
    wide = jnp.concatenate(
        [jnp.where(head_row == k, query_float, 0.0) for k in range(kv_heads)], axis=1).astype(jnp.bfloat16)
    load_c.wait()
    kv_cols = kv_heads * HD
    scores = lax.dot_general(wide, cache[:, 0:kv_cols], (((1,), (1,)), ((), ())),
                             preferred_element_type=jnp.float32) * scale
    usable = lax.broadcasted_iota(jnp.int32, scores.shape, 1) < seq_len
    scores = jnp.where(usable, scores, jnp.float32(-1e30))
    largest = jnp.maximum(jnp.max(scores, axis=1, keepdims=True), own_score)
    exponent = jnp.where(usable, jnp.exp(scores - largest), 0.0)
    own_exp = jnp.exp(own_score - largest)
    inv_total = 1.0 / (jnp.sum(exponent, axis=1, keepdims=True) + own_exp)
    probs = (exponent * inv_total).astype(jnp.bfloat16)
    own_prob = (own_exp * inv_total).astype(jnp.bfloat16).astype(jnp.float32)
    mixed = jnp.dot(probs, cache[:, kv_cols:2 * kv_cols], preferred_element_type=jnp.float32)
    picked = jnp.concatenate(
        [mixed[k * per_kv:(k + 1) * per_kv, k * HD:(k + 1) * HD] for k in range(kv_heads)], axis=0)
    attended = picked + own_prob * per_query(new_value)
    for j in range(q_heads):
        out_ref[0, 0, :, j * HD:(j + 1) * HD] = attended[j:j + 1].astype(jnp.bfloat16)

    for p in plane:
        copy_a(p, me, me).wait_send()
        copy_p(p, me, me).wait_send()
    for z in line:
        copy_b(z, t, t).wait_send()
        copy_z(z, t, t).wait_send()


def shards(sizes, hidden_states, query_train, keyval_train, layer_of_section, lengths, kv_cache):
    n_group, n_section, n_tensor = sizes
    n_plane = n_group * n_section
    d = hidden_states.shape[-1]
    layers, rows, q_cols = query_train.shape
    k_cols = keyval_train.shape[2]
    kv_len, kv_width = kv_cache.shape[-2:]
    q_heads = q_cols * n_tensor // HD
    kv2 = kv_width // HD
    bf16 = jnp.bfloat16
    hbm = pl.BlockSpec(memory_space=pltpu.HBM)
    anym = pl.BlockSpec(memory_space=pl.ANY)
    vmem = pl.BlockSpec(memory_space=pltpu.VMEM)
    dma = pltpu.SemaphoreType.DMA
    return pl.pallas_call(
        functools.partial(kernel, sizes),
        out_shape=(pltpu.VMEM((1, 1, 1, q_heads * HD), bf16), pltpu.VMEM((1, 1, 1, kv_width), bf16)),
        in_specs=[hbm, hbm, anym, anym, anym, anym],
        out_specs=(vmem, vmem),
        scratch_shapes=[
            pltpu.SMEM(layer_of_section.shape, jnp.int32),
            pltpu.SMEM(lengths.shape, jnp.int32),
            pltpu.VMEM((1, d), bf16),
            pltpu.VMEM((d // HD, HD), jnp.float32),
            pltpu.VMEM((n_plane, rows // HD, HD), bf16),
            pltpu.VMEM((n_tensor, n_plane, rows // HD, HD), bf16),
            pltpu.VMEM((n_section, n_group * n_tensor * (rows // HD), HD), jnp.float32),
            pltpu.VMEM((layers, rows, q_cols), bf16),
            pltpu.VMEM((layers, rows, k_cols), bf16),
            pltpu.VMEM((kv_len, kv_width), bf16),
            pltpu.VMEM((n_plane, n_tensor, q_cols + k_cols), bf16),
            pltpu.VMEM((n_plane, n_tensor, q_cols + k_cols), bf16),
            pltpu.VMEM((n_tensor, 1, q_cols + k_cols), bf16),
            pltpu.VMEM((n_tensor, 1, q_cols + k_cols), bf16),
            pltpu.VMEM((q_heads + kv2, HD), jnp.float32),
            dma((2,)), dma, dma((2, layers)), dma,
            dma((n_plane,)), dma((n_plane,)), dma((n_tensor,)), dma((n_tensor,)),
            dma((n_plane,)), dma((n_plane,)), dma((n_tensor,)), dma((n_tensor,)),
        ],
        compiler_params=pltpu.CompilerParams(collective_id=0, has_side_effects=True),
    )(layer_of_section, lengths, hidden_states.reshape(1, d), query_train, keyval_train,
      kv_cache.reshape(kv_len, kv_width))


def solution(mesh):
    sizes = (mesh.shape["group"], mesh.shape["section"], mesh.shape["tensor"])
    in_specs = (
        P("group", "section", "tensor", None),
        P(None, ("group", "section"), "tensor"),
        P(None, ("group", "section"), "tensor"),
        P(),
        P("group", "section", "tensor"),
        P("group", "section", "tensor", None, None),
    )
    out_specs = (P("group", "section", "tensor", None), P("group", "section", "tensor", None))
    return jax.shard_map(
        functools.partial(shards, sizes), mesh=mesh, in_specs=in_specs, out_specs=out_specs, check_vma=False)
```

time: 192 us -> 25.2 us (0.13)
  waiting for transfers between devices: 97.8 us -> 0 us
  local copies, waits for them, and re-layouts: 28.1 us -> 1.2 us
  blocking collectives: 23 us -> 0 us
  Pallas kernels: 0 us -> 22.6 us
  starting transfers between devices: 21.6 us -> 0 us
  other arithmetic: 11.8 us -> 0 us
  matrix products: 7.11 us -> 0 us
    all_to_all x5 -> x0, waiting for transfers between devices: 97.8 us -> none  [the longest x1 85.2 us: shards(): lax.all_to_all(query_sorted, 'section', split_axis=0, concat_axis=1, tile...]
    pallas_call x0 -> x1, Pallas kernels: none -> 22.6 us  [shards(): pl.pallas_call(functools.partial(kernel, sizes), out_shape=(pltpu.VMEM((1...]
    all_to_all x5 -> x0, starting transfers between devices: 21.6 us -> none  [the longest x1 5.67 us: shards(): lax.all_to_all(query_sorted, 'section', split_axis=0, concat_axis=1, tile...]
    gather x4 -> x0, local copies, waits for them, and re-layouts: 17.8 us -> none  [the longest x3 15.8 us: shards(): query_sorted = query_train[layer_of_section]]
    all_gather x1 -> x0, blocking collectives: 15.4 us -> none  [shards(): lax.all_gather(hidden_states[0, 0], 'tensor', axis=0, tiled=True)]
    unnamed x2 -> x0, other arithmetic: 7.75 us -> none
    unnamed x1 -> x0, blocking collectives: 7.55 us -> none
    dot_general x4 -> x0, matrix products: 7.11 us -> none  [the longest x1 4.88 us: shards(): jnp.einsum('gbr,rc->gbc', arrived[:, :, 0, :], w_both, preferred_element_...]
  transfers between devices with their start and end apart: 5 -> 0, of which waited for: 5 -> 0; matrix products, arithmetic and copies ran while one was open for 19% -> 0% of each run, Pallas kernels for 0% -> 0%
where the time goes in v1:
time: 25.2 us; the launch traced here: 25.1 us
  Pallas kernels  22.6 us (90%)
  between operations  1.29 us (5%)
  local copies, waits for them, and re-layouts  1.2 us (5%)
    pallas_call x1, Pallas kernels, shards(): pl.pallas_call(functools.partial(kernel, sizes), out_shape=(pltpu.VMEM((1...  22.6 us
    unnamed x2, local copies, waits for them, and re-layouts  1.2 us

profile of v1, /device:TPU:0, one launch (start us, length us, event | category | flops | bytes accessed | tf_op | source)
XLA Modules:
  0.0 25.1 jit_solution(9778471913027903978)
XLA Ops:
  1.3 22.6 %shard_map.77 = (bf16[1,1,1,4096]{3,2,1,0:T(2,128)(2,1)S(1)}, bf16[1,1,1,1024]{3,2,1,0:T(2,128)(2,1)S(1)}) custom-call(s32[4]{0:T(128)} %layer_hbm.1, s32[1,1,1]{2,1,0:T(1,128)S(6)} %copy.12.len_hbm, bf16[1,8192]{1,0:T(2,128)(2,1)} %bitcast.3, bf16[4,1024,1024]{2,1,0:T(8,128)(2,1)} %wq_hbm.1, bf16[4,1024,256]{2,1,0:T(8,128)(2,1)} %wk_hbm.1, ...), custom_call_target="tpu_custom_call" | custom-call | tf_op jit(solution)/shard_map/pallas_call | solution.py:234
  23.9 0.6 %copy.10 = bf16[1,1,1,4096]{3,2,1,0:T(2,128)(2,1)} copy(bf16[1,1,1,4096]{3,2,1,0:T(2,128)(2,1)S(1)} %get-tuple-element.2) | data formatting | bytes 16384
  24.5 0.6 %copy.11 = bf16[1,1,1,1024]{3,2,1,0:T(2,128)(2,1)} copy(bf16[1,1,1,1024]{3,2,1,0:T(2,128)(2,1)S(1)} %get-tuple-element.3) | data formatting | bytes 4096
